TPU v7x, 256 devices: a whole 4x4x8 slice. The times are simulated.
256 devices in a mesh: heads: 8 (over y, core), tok: 32 (over x, z).
Axes of the slice: x: 4, y: 4, z: 8, core: 2. Of those that a mesh axis runs over, the one named last changes fastest.
Arguments:
- video_q: bfloat16 [32768, 2048], P('tok', 'heads'), as said below
- video_k: bfloat16 [32768, 2048], P('tok', 'heads'), as said below
- video_v: bfloat16 [32768, 2048], P('tok', 'heads'), may hold values from -6 to 6
- audio_q: bfloat16 [2048, 2048], P('tok', 'heads'), as said below
- audio_k: bfloat16 [2048, 2048], P('tok', 'heads'), as said below
- audio_v: bfloat16 [2048, 2048], P('tok', 'heads'), may hold values from -6 to 6
- video_q_gain: float32 [2048], P('heads'), may hold values from 0.1 to 1.9
- audio_k_gain: float32 [2048], P('heads'), may hold values from 0.1 to 1.9
- audio_q_gain: float32 [2048], P('heads'), may hold values from 0.1 to 1.9
- video_k_gain: float32 [2048], P('heads'), may hold values from 0.1 to 1.9
Outputs:
- video_out: bfloat16 [32768, 2048], P('tok', 'heads')
- audio_out: bfloat16 [2048, 2048], P('tok', 'heads')
Inputs may be any that keep to these rules, and one draw needn't show every extreme that they name: `video_q`: no row is zero. `video_k`: no row is zero. `audio_q`: no row is zero. `audio_k`: no row is zero.
All inputs are finite; a program needn't handle non-finite values.
Results may differ from a plain program's by a relative error of at most 0.012.
The roundings to bfloat16 on the way count: a program that leaves them out, or rounds other values in their place, can miss the bound.
Values may be sent and summed in bfloat16 or wider, within the bound.
A program may use at most 64 MiB of HBM per device.

v0:
```python
import math

import jax
import jax.numpy as jnp
from jax import lax
from jax.sharding import PartitionSpec as P

HEADS = 32
HD = 64


EPS = 1e-06


def from_everyone(value, axis):
    peers = lax.axis_size(axis)
    return lax.all_to_all(
        jnp.broadcast_to(value[None], (peers, *value.shape)), axis, 0, 0, tiled=True
    )


def taken_together(value, axis):
    return from_everyone(value, axis).sum(axis=0)


def together(arrays, axis):
    ends = [0]
    for a in arrays:
        ends.append(ends[-1] + a.size)
    so_far = taken_together(jnp.concatenate([a.ravel() for a in arrays]), axis)
    return tuple((so_far[b:e].reshape(a.shape) for a, b, e in zip(arrays, ends, ends[1:])))


def sent_together(arrays, axis, dim, along):
    both = jnp.concatenate(arrays, axis=along)
    whole, at, done = (lax.all_gather(both, axis, axis=dim, tiled=True), 0, [])
    for a in arrays:
        done.append(lax.slice_in_dim(whole, at, at + a.shape[along], axis=along))
        at += a.shape[along]
    return tuple(done)


def squares(rows):
    values = rows.astype(jnp.float32)
    return jnp.sum(values * values, axis=1)


def normalize(rows, summed, gain):
    scaled = lax.rsqrt(summed / (HEADS * HD) + EPS)[:, None]
    return (rows.astype(jnp.float32) * scaled * gain).astype(jnp.bfloat16)


def body(
    video_q,
    video_k,
    video_v,
    audio_q,
    audio_k,
    audio_v,
    video_q_gain,
    audio_k_gain,
    audio_q_gain,
    video_k_gain,
):
    factor = HD ** (-0.5)
    tok_rows = video_q.shape[0]
    aud_rows = audio_q.shape[0]
    local_width = video_q.shape[1]
    local_heads = local_width // HD
    sum_vq, sum_ak, sum_aq, sum_vk = together(
        (squares(video_q), squares(audio_k), squares(audio_q), squares(video_k)), "heads"
    )
    query_v = normalize(video_q, sum_vq, video_q_gain)
    key_a = normalize(audio_k, sum_ak, audio_k_gain)
    query_a = normalize(audio_q, sum_aq, audio_q_gain)
    key_v = normalize(video_k, sum_vk, video_k_gain)
    key_all, value_all, query_all = sent_together((key_a, audio_v, query_a), "tok", 0, 1)
    audio_total = key_all.shape[0]
    key_heads = key_all.reshape(audio_total, local_heads, HD)
    value_heads = value_all.reshape(audio_total, local_heads, HD)
    block = math.gcd(tok_rows, 512)
    count = tok_rows // block

    def first(pair):
        query, value = pair
        scores = (
            jnp.einsum(
                "qhd,khd->hqk",
                query.reshape(block, local_heads, HD),
                key_heads,
                preferred_element_type=jnp.float32,
            )
            * factor
        )
        top = jnp.max(scores, axis=-1, keepdims=True)
        expo = jnp.exp(scores - top)
        total = jnp.sum(expo, axis=-1)
        weights = expo.astype(jnp.bfloat16)
        mixed = (
            jnp.einsum("hqk,khd->qhd", weights, value_heads, preferred_element_type=jnp.float32)
            / jnp.transpose(total)[:, :, None]
        )
        return (value.astype(jnp.float32) + mixed.reshape(block, local_width)).astype(jnp.bfloat16)

    video_out = lax.map(
        first,
        (query_v.reshape(count, block, local_width), video_v.reshape(count, block, local_width)),
    ).reshape(tok_rows, local_width)
    key_local = key_v.reshape(tok_rows, local_heads, HD)
    value_local = video_out.reshape(tok_rows, local_heads, HD)
    rows_block = math.gcd(audio_total, 512)
    rows_count = audio_total // rows_block

    def second(query):
        scores = (
            jnp.einsum(
                "qhd,khd->hqk",
                query.reshape(rows_block, local_heads, HD),
                key_local,
                preferred_element_type=jnp.float32,
            )
            * factor
        )
        top = jnp.max(scores, axis=-1)
        expo = jnp.exp(scores - top[:, :, None])
        total = jnp.sum(expo, axis=-1)
        weights = expo.astype(jnp.bfloat16)
        part = jnp.einsum("hqk,khd->qhd", weights, value_local, preferred_element_type=jnp.float32)
        return (part, jnp.transpose(top), jnp.transpose(total))

    partial_value, tops, totals = lax.map(
        second, query_all.reshape(rows_count, rows_block, local_width)
    )
    partial_value = partial_value.reshape(audio_total, local_heads, HD)
    tops = tops.reshape(audio_total, local_heads)
    totals = totals.reshape(audio_total, local_heads)
    got_part, got_top, got_total = (
        lax.all_to_all(partial_value, "tok", split_axis=0, concat_axis=0, tiled=True),
        lax.all_to_all(tops, "tok", split_axis=0, concat_axis=0, tiled=True),
        lax.all_to_all(totals, "tok", split_axis=0, concat_axis=0, tiled=True),
    )
    senders = got_part.shape[0] // aud_rows
    got_part = got_part.reshape(senders, aud_rows, local_heads, HD)
    got_top = got_top.reshape(senders, aud_rows, local_heads)
    got_total = got_total.reshape(senders, aud_rows, local_heads)
    highest = jnp.max(got_top, axis=0)
    scale_rows = jnp.exp(got_top - highest[None])
    summed = jnp.sum(got_part * scale_rows[:, :, :, None], axis=0)
    denominator = jnp.sum(got_total * scale_rows, axis=0)
    audio_out = (
        (summed / denominator[:, :, None]).reshape(aud_rows, local_width).astype(jnp.bfloat16)
    )
    return (video_out, audio_out)


def solution(mesh):
    return jax.shard_map(
        body,
        mesh=mesh,
        in_specs=(
            P("tok", "heads"),
            P("tok", "heads"),
            P("tok", "heads"),
            P("tok", "heads"),
            P("tok", "heads"),
            P("tok", "heads"),
            P("heads"),
            P("heads"),
            P("heads"),
            P("heads"),
        ),
        out_specs=(P("tok", "heads"), P("tok", "heads")),
        check_vma=False,
    )
```

profile of v0, /device:TPU:32, one launch (start us, length us, event | category | flops | bytes accessed | tf_op | source)
XLA Modules:
  0.0 290.1 jit_solution(16688094642769501763)
XLA Ops:
  9.8 9.9 %all_to_all.29 = f32[8,1,2176]{2,1,0:T(1,128)S(1)} all-to-all(f32[8,1,2176]{2,1,0:T(1,128)S(1)} %broadcast_in_dim.20), channel_id=1, replica_groups=mesh['heads'=8,'tok'=32] {'heads'}, dimensions={0} | all-to-all | bytes 139264 | tf_op jit(solution)/shard_map/all_to_all | solution.py:17
  25.7 76.8 %all-gather.2.cloned.1.call-done = bf16[2048,768]{1,0:T(8,128)(2,1)} async-done(((bf16[64,768]{1,0:T(8,128)(2,1)}), bf16[2048,768]{1,0:T(8,128)(2,1)}) %all-gather.2.cloned.1.call-update) | async-done | bytes 3145744 | tf_op jit(solution)/shard_map/all_gather | solution.py:36
  102.5 3.4 %fusion.43 = (bf16[2048,256]{1,0:T(8,128)(2,1)}, bf16[2048,256]{1,0:T(8,128)(2,1)}, bf16[2048,256]{1,0:T(8,128)(2,1)S(1)}) fusion(bf16[2048,768]{1,0:T(8,128)(2,1)} %all-gather.2.cloned.1.call-done), kind=kLoop, calls=%fused_computation.59 | loop fusion | bytes 6291456 | tf_op jit(solution)/shard_map/slice | solution.py:38
  108.8 35.9 %while.24 = (s32[]{:T(128)}, bf16[2,512,256]{1,2,0:T(8,128)(2,1)}, bf16[2,512,256]{2,1,0:T(8,128)(2,1)}, bf16[2,512,256]{2,1,0:T(8,128)(2,1)S(1)}, bf16[2048,4,6...) while((s32[]{:T(128)}, bf16[2,512,256]{1,2,0:T(8,128)(2,1)}, ...), condition=%wide.region_8.9_spmd, body=%wide.region_5.8_spmd.sunk | while | flops 1107816448 | bytes 123511400 | solution.py:105
  112.4 3.3 %fusion.66 = f32[4,512]{1,0:T(4,128)S(1)} fusion(f32[4,512,2048]{2,1,0:T(8,128)S(1)} %get-tuple-element.273, f32[4,512]{1,0:T(4,128)S(1)} %get-tuple-element.274), kind=kLoop, calls=%fused_computation.2.clone.1 | loop fusion | flops 12580864 | bytes 16793600 | tf_op jit(solution)/shard_map/while/body/eval_jaxpr/reduce_sum | solution.py:97
  118.1 7.7 %fusion.67 = f32[512,4,64]{0,2,1:T(8,128)S(1)} fusion(bf16[2048,4,64]{0,2,1:T(8,128)(2,1)} %get-tuple-element.304, f32[4,512,2048]{2,1,0:T(8,128)} %copy-done, f32[4,512]{1,0:T(4,128)S(1)} %get-tuple-element.274, f32[512,4]{0,1:T(4,128)S(1)} %bitcast.98), kind=kOutput, calls=%fused_computation.6.clone.1 | convolution fusion | flops 549584896 | bytes 18366464 | tf_op jit(solution)/shard_map/while/body/eval_jaxpr/hqk,khd->qhd/dot_general | solution.py:100
  130.4 3.3 %fusion.66 = f32[4,512]{1,0:T(4,128)S(1)} fusion(f32[4,512,2048]{2,1,0:T(8,128)S(1)} %get-tuple-element.273, f32[4,512]{1,0:T(4,128)S(1)} %get-tuple-element.274), kind=kLoop, calls=%fused_computation.2.clone.1 | loop fusion | flops 12580864 | bytes 16793600 | tf_op jit(solution)/shard_map/while/body/eval_jaxpr/reduce_sum | solution.py:97
  136.1 7.7 %fusion.67 = f32[512,4,64]{0,2,1:T(8,128)S(1)} fusion(bf16[2048,4,64]{0,2,1:T(8,128)(2,1)} %get-tuple-element.304, f32[4,512,2048]{2,1,0:T(8,128)} %copy-done, f32[4,512]{1,0:T(4,128)S(1)} %get-tuple-element.274, f32[512,4]{0,1:T(4,128)S(1)} %bitcast.98), kind=kOutput, calls=%fused_computation.6.clone.1 | convolution fusion | flops 549584896 | bytes 18366464 | tf_op jit(solution)/shard_map/while/body/eval_jaxpr/hqk,khd->qhd/dot_general | solution.py:100
  146.7 28.4 %while.25 = (s32[]{:T(128)}, f32[4,512,4,64]{1,3,2,0:T(8,128)}, f32[4,512,4]{1,0,2:T(4,128)S(1)}, f32[4,512,4]{1,0,2:T(4,128)S(1)}, bf16[4,512,256]{2,1,0:T(8,12...) while((s32[]{:T(128)}, f32[4,512,4,64]{1,3,2,0:T(8,128)}, ...), condition=%wide.region_12.13_spmd, body=%wide.region_9.12_spmd.sunk | while | flops 553644032 | bytes 28148328 | solution.py:131
  149.2 2.6 fusion.72
  156.3 2.6 fusion.72
  163.4 2.6 fusion.72
  170.5 2.6 fusion.72
  176.0 6.0 %all-to-all-start.2 = ((f32[32,1,256]{2,1,0:T(1,128)}), f32[32,1,256]{2,1,0:T(1,128)S(1)}, u32[]{:S(2)}, u32[]{:S(2)}) async-start(f32[32,1,256]{2,1,0:T(1,128)} %reshape.95), calls=%async_computation.2 | async-start | bytes 65536 | tf_op jit(solution)/shard_map/all_to_all | solution.py:139
  182.8 8.0 %all-to-all-done.2 = f32[32,1,256]{2,1,0:T(1,128)S(1)} async-done(((f32[32,1,256]{2,1,0:T(1,128)}), f32[32,1,256]{2,1,0:T(1,128)S(1)}, u32[]{:S(2)}, u32[]{:S(2)}) %all-to-all-start.2) | async-done | bytes 32800 | tf_op jit(solution)/shard_map/all_to_all | solution.py:139
  190.8 4.8 %all-to-all-start.3 = ((f32[32,1,256]{2,1,0:T(1,128)}), f32[32,1,256]{2,1,0:T(1,128)S(1)}, u32[]{:S(2)}, u32[]{:S(2)}) async-start(f32[32,1,256]{2,1,0:T(1,128)} %reshape.97), calls=%async_computation.3 | async-start | bytes 65536 | tf_op jit(solution)/shard_map/all_to_all | solution.py:140
  195.6 4.8 %copy.96 = f32[4,512,4,64]{3,2,1,0:T(4,128)} copy(f32[4,512,4,64]{1,3,2,0:T(8,128)} %get-tuple-element.74) | data formatting | bytes 4194304 | tf_op jit(solution)/shard_map/reshape | solution.py:134
  200.4 6.3 %reshape.93 = f32[32,1,16384]{2,1,0:T(1,128)} reshape(f32[2048,4,64]{2,1,0:T(4,128)} %bitcast.86) | data formatting | bytes 4194304
  206.7 10.0 %all-to-all-start.1 = ((f32[32,1,16384]{2,1,0:T(1,128)}), f32[32,1,16384]{2,1,0:T(1,128)}, u32[]{:S(2)}, u32[]{:S(2)}) async-start(f32[32,1,16384]{2,1,0:T(1,128)} %reshape.93), calls=%async_computation.1 | async-start | bytes 4194304 | tf_op jit(solution)/shard_map/all_to_all | solution.py:138
  219.9 42.5 %all-to-all-done.1 = f32[32,1,16384]{2,1,0:T(1,128)} async-done(((f32[32,1,16384]{2,1,0:T(1,128)}), f32[32,1,16384]{2,1,0:T(1,128)}, u32[]{:S(2)}, u32[]{:S(2)}) %all-to-all-start.1) | async-done | bytes 2097184 | tf_op jit(solution)/shard_map/all_to_all | solution.py:138
  262.5 7.4 %reduce.2 = f32[32,16384]{1,0:T(8,128)S(1)} reduce(f32[32,1,16384]{2,1,0:T(1,128)} %all-to-all-done.1, f32[]{:T(128)} %broadcast.74), dimensions={1}, to_apply=%all_to_all.20.reduce_sub_computation | reduce | bytes 4194308 | tf_op jit(solution)/shard_map/all_to_all | solution.py:138
  269.9 4.2 %reshape.94 = f32[2048,4,64]{2,1,0:T(4,128)} reshape(f32[32,16384]{1,0:T(8,128)S(1)} %reduce.2) | data formatting | bytes 4194304
  274.1 5.4 %copy.91 = f32[32,64,4,64]{1,0,3,2:T(8,128)} copy(f32[32,64,4,64]{3,2,1,0:T(4,128)} %bitcast.87) | data formatting | bytes 4194304 | tf_op jit(solution)/shard_map/reshape | solution.py:143
  279.4 3.1 %multiply_reduce_fusion.2 = f32[64,4,64]{0,2,1:T(8,128)S(1)} fusion(f32[32,64,4,64]{1,0,3,2:T(8,128)} %copy.91, f32[32,64,4]{1,0,2:T(8,128)S(1)} %copy.90), kind=kLoop, calls=%fused_computation.22 | loop fusion | flops 1032192 | bytes 2195456 | tf_op jit(solution)/shard_map/reduce_sum | solution.py:148
  (89 shorter events, 50.8 us)
Async XLA Ops:
  7.2 95.3 %all-gather.2.cloned.1.call-start = ((), (), s32[]{:S(2)}) async-start(), calls=%async_computation.4 | async-start | bytes 3244032 | tf_op jit(solution)/shard_map/all_gather | solution.py:36
  112.4 5.7 %copy-start = (f32[4,512,2048]{2,1,0:T(8,128)}, f32[4,512,2048]{2,1,0:T(8,128)S(1)}, u32[]{:S(2)}) copy-start(f32[4,512,2048]{2,1,0:T(8,128)S(1)} %get-tuple-element.273) | copy-start | bytes 50331652 | tf_op jit(solution)/shard_map/while
  130.4 5.7 %copy-start = (f32[4,512,2048]{2,1,0:T(8,128)}, f32[4,512,2048]{2,1,0:T(8,128)S(1)}, u32[]{:S(2)}) copy-start(f32[4,512,2048]{2,1,0:T(8,128)S(1)} %get-tuple-element.273) | copy-start | bytes 50331652 | tf_op jit(solution)/shard_map/while
  176.0 14.9 %all-to-all-start.2 = ((f32[32,1,256]{2,1,0:T(1,128)}), f32[32,1,256]{2,1,0:T(1,128)S(1)}, u32[]{:S(2)}, u32[]{:S(2)}) async-start(f32[32,1,256]{2,1,0:T(1,128)} %reshape.95), calls=%async_computation.2 | async-start | bytes 65536 | tf_op jit(solution)/shard_map/all_to_all | solution.py:139
  190.8 15.9 %all-to-all-start.3 = ((f32[32,1,256]{2,1,0:T(1,128)}), f32[32,1,256]{2,1,0:T(1,128)S(1)}, u32[]{:S(2)}, u32[]{:S(2)}) async-start(f32[32,1,256]{2,1,0:T(1,128)} %reshape.97), calls=%async_computation.3 | async-start | bytes 65536 | tf_op jit(solution)/shard_map/all_to_all | solution.py:140
  195.6 21.1 %copy-start.1 = (bf16[2,512,256]{1,2,0:T(8,128)(2,1)S(1)}, bf16[2,512,256]{1,2,0:T(8,128)(2,1)}, u32[]{:S(2)}) copy-start(bf16[2,512,256]{1,2,0:T(8,128)(2,1)} %get-tuple-element.73) | copy-start | bytes 1572868
  206.7 55.8 %all-to-all-start.1 = ((f32[32,1,16384]{2,1,0:T(1,128)}), f32[32,1,16384]{2,1,0:T(1,128)}, u32[]{:S(2)}, u32[]{:S(2)}) async-start(f32[32,1,16384]{2,1,0:T(1,128)} %reshape.93), calls=%async_computation.1 | async-start | bytes 4194304 | tf_op jit(solution)/shard_map/all_to_all | solution.py:138
Sparse Core Ops, SparseCore 0:
  23.1 79.3 all-gather.1
where the time goes:
time: 292 us; the launch traced here: 290 us
  waiting for transfers between devices  127 us (43%)
  local copies, waits for them, and re-layouts  45.8 us (16%)
  matrix products  36.3 us (12%)
  other arithmetic  35.5 us (12%)
  starting transfers between devices  20.8 us (7%)
  between operations  14.2 us (5%)
  blocking collectives  9.91 us (3%)
    all_gather x1, waiting for transfers between devices, sent_together(): whole, at, done = (lax.all_gather(both, axis, axis=dim, tiled=True), 0, [])  76.8 us
    all_to_all x1, waiting for transfers between devices, body(): lax.all_to_all(partial_value, 'tok', split_axis=0, concat_axis=0, tiled=T...  42.5 us
    unnamed x11, local copies, waits for them, and re-layouts  15.7 us
    dot_general x2, matrix products, first(): jnp.einsum('hqk,khd->qhd', weights, value_heads, preferred_element_type=j...  15.4 us
    dot_general x4, matrix products, second(): jnp.einsum('hqk,khd->qhd', weights, value_local, preferred_element_type=j...  10.4 us
    all_to_all x1, starting transfers between devices, body(): lax.all_to_all(partial_value, 'tok', split_axis=0, concat_axis=0, tiled=T...  9.95 us
    all_to_all x1, blocking collectives, from_everyone(): lax.all_to_all(jnp.broadcast_to(value[None], (peers, *value.shape)), axis...  9.91 us
    all_to_all x1, waiting for transfers between devices, body(): lax.all_to_all(tops, 'tok', split_axis=0, concat_axis=0, tiled=True)  7.99 us
  transfers between devices with their start and end apart: 4, of which 3 were waited for; matrix products, arithmetic and copies ran while one was open for 6% of the time, Pallas kernels for 0%

commit v1 on v0

v1 whole, which is shorter than its diff:
```python
import functools
import jax
import jax.numpy as jnp
from jax import lax
from jax.experimental import pallas as pl
from jax.experimental.pallas import tpu as pltpu
from jax.sharding import PartitionSpec as P

HEADS = 32
HD = 64
EPS = 1e-06
LOG2E = 1.4426950408889634
NX, NZ, NH = 4, 8, 8
NT = (((1,), (1,)), ((), ()))
BF = jnp.bfloat16
F32 = jnp.float32
MESH = pl.DeviceIdType.MESH
TQ = 256
TK = 512


def make_rhs(q_ref, row0, rows, h, factor):
    pair = pl.multiple_of((h // 2) * 128, 128)
    x = q_ref[pl.ds(row0, rows), pl.ds(pair, 128)].astype(F32) * factor
    lane = lax.broadcasted_iota(jnp.int32, (rows, 128), 1)
    x = jnp.where((lane // HD) == (h % 2), x, 0.0)
    hi = x.astype(BF)
    lo = (x - hi.astype(F32)).astype(BF)
    return jnp.concatenate([hi, lo], axis=1)


def scores_step(k_ref, h, kt, tk, rhs, s_ref, m):
    pair = pl.multiple_of((h // 2) * 128, 128)
    kk = k_ref[pl.ds(kt * tk, tk), pl.ds(pair, 128)]
    s = lax.dot_general(jnp.concatenate([kk, kk], axis=1), rhs, NT, preferred_element_type=F32)
    s_ref[pl.ds(kt * tk, tk), :] = s
    part = jnp.max(s.reshape(tk // 8, 8, s.shape[1]), axis=0)
    return part if m is None else jnp.maximum(m, part)


def mix_step(v_ref, h, kt, tk, s_ref, m, acc):
    p = jnp.exp2(s_ref[pl.ds(kt * tk, tk), :] - m).astype(BF)
    part = jnp.dot(v_ref[h, :, pl.ds(kt * tk, tk)], p, preferred_element_type=F32)
    return part if acc is None else acc + part


def attend(n_items, item, k_ref, v_ref, q_ref, keys, tk, tq, factor, s_refs, m_refs, finish):
    steps = keys // tk

    def scores(i, s_ref, m_ref, mix=None):
        h, row0 = item(i)
        rhs = make_rhs(q_ref, row0, tq, h, factor)
        m, acc = None, None
        for kt in range(steps):
            m = scores_step(k_ref, h, kt, tk, rhs, s_ref, m)
            if mix is not None:
                acc = mix_step(v_ref, mix[0], kt, tk, mix[2], mix[1], acc)
        m_ref[...] = jnp.broadcast_to(jnp.max(m, axis=0, keepdims=True), (8, tq))
        return acc

    def one(i, now, prev):
        h, row0 = item(i - 1)
        mprev = m_refs[prev][0:1]
        acc = scores(i, s_refs[now], m_refs[now], (h, mprev, s_refs[prev]))
        finish(i - 1, h, row0, acc, mprev)

    scores(0, s_refs[0], m_refs[0])

    def body(j, c):
        one(2 * j + 1, 1, 0)
        one(2 * j + 2, 0, 1)
        return c

    lax.fori_loop(0, n_items // 2 - 1, body, 0)
    one(n_items - 1, 1, 0)
    h, row0 = item(n_items - 1)
    mprev = m_refs[1][0:1]
    acc = None
    for kt in range(steps):
        acc = mix_step(v_ref, h, kt, tk, s_refs[1], mprev, acc)
    finish(n_items - 1, h, row0, acc, mprev)


def row_sums(x):
    x = x.astype(F32)
    y = x[:, :128] * x[:, :128] + x[:, 128:] * x[:, 128:]
    return jnp.sum(jnp.transpose(y), axis=0, keepdims=True)


def along_rows(row):
    return jnp.transpose(jnp.broadcast_to(row, (128, 128)))


def scaled(x, col, gain):
    c = jnp.concatenate([col, col], axis=1)
    return (x.astype(F32) * c * gain).astype(BF)


def kernel(vq_h, vk_h, vv_h, aq_h, ak_h, av_h, gvq, gak, gaq, gvk, vout_h, aout,
           vq, vk, vv, araw, va, ka, qa, vT, voT, vvT, sa, sb, ma, mb,
           st_own, st_all, pT, xrecv, lse, lrecv, zsend, zrecv, lsend, lzrecv, vout,
           in_sem, out_sem, st_send, st_recv, g_send, g_recv, x_send, x_recv, xl_send, xl_recv, z_send, z_recv, zl_send, zl_recv):
    hx = lax.axis_index("heads")
    tok = lax.axis_index("tok")
    x0, z0 = tok // NZ, tok % NZ
    n, na, ar = vq.shape[0], ka.shape[0], araw.shape[1]

    def at(x, z):
        return (x % NX) * NZ + (z % NZ)

    ins = [pltpu.make_async_copy(vq_h, vq, in_sem.at[0]), pltpu.make_async_copy(vk_h, vk, in_sem.at[1]),
           pltpu.make_async_copy(aq_h, araw.at[1], in_sem.at[2]), pltpu.make_async_copy(ak_h, araw.at[0], in_sem.at[3]),
           pltpu.make_async_copy(av_h, va.at[pl.ds(pl.multiple_of(tok * ar, ar), ar)], in_sem.at[4]),
           pltpu.make_async_copy(vv_h, vv, in_sem.at[5])]
    for c in ins:
        c.start()

    peers = [{"heads": (hx + i) % NH} for i in range(1, NH)]
    peers += [{"tok": at(x0 + i, z0)} for i in range(1, NX)] + [{"tok": at(x0, z0 + i)} for i in range(1, NZ)]
    barrier = pltpu.get_barrier_semaphore()
    for p in peers:
        pl.semaphore_signal(barrier, inc=1, device_id=p, device_id_type=MESH)
    pl.semaphore_wait(barrier, len(peers))

    def gather(buf, t, zfirst):
        np_, ns = (NZ, NX) if zfirst else (NX, NZ)
        p0, s0 = (z0, x0) if zfirst else (x0, z0)

        def dev(p, s):
            return at(s, p) if zfirst else at(p, s)

        def block(b):
            return buf.at[pl.ds(pl.multiple_of(b * ar, ar), ar)]

        def send(b, to):
            pltpu.make_async_remote_copy(src_ref=block(b), dst_ref=block(b), send_sem=g_send.at[t], recv_sem=g_recv.at[t, b],
                                         device_id={"tok": to}, device_id_type=MESH).start()

        def recv(b):
            pltpu.make_async_copy(block(b), block(b), g_recv.at[t, b]).wait()

        def spread(p):
            send(dev(p, s0), dev(p0, s0 + 1))
            send(dev(p, s0), dev(p0, s0 - 1))

        half, shalf = np_ // 2, ns // 2
        sgn_s = 1 - 2 * (s0 % 2)
        steps = []

        def first():
            send(dev(p0, s0), dev(p0 + 1, s0))
            send(dev(p0, s0), dev(p0 - 1, s0))
            spread(p0)

        steps.append(first)
        for i in range(1, half):
            def prim(i=i):
                for d in (1, -1):
                    b = dev(p0 - d * i, s0)
                    recv(b)
                    if i < half - 1:
                        send(b, dev(p0 + d, s0))
                if i == half - 1:
                    send(dev(p0 - sgn_s * i, s0), dev(p0 + sgn_s, s0))
                for d in (1, -1):
                    spread(p0 - d * i)
            steps.append(prim)

        def opposite():
            recv(dev(p0 + half, s0))
            spread(p0 + half)

        steps.append(opposite)
        order = [0] + [o for i in range(1, half) for o in (-i, i)] + [half]
        for j in range(1, shalf):
            for o in order:
                def sec(o=o, j=j):
                    p = p0 + o
                    for d in (1, -1):
                        b = dev(p, s0 - d * j)
                        recv(b)
                        if j < shalf - 1:
                            send(b, dev(p0, s0 + d))
                    if j == shalf - 1:
                        d = 1 - 2 * ((p0 + o + np_) % 2)
                        send(dev(p, s0 - d * j), dev(p0, s0 + d))
                steps.append(sec)
        for o in order:
            steps.append(lambda o=o: recv(dev(p0 + o, s0 + shalf)))
        return steps

    def drain(buf, t):
        rows = buf.at[pl.ds(0, (NX * NZ - 1) * ar)]
        pltpu.make_async_copy(rows, rows, g_send.at[t]).wait()

    ins[4].wait()
    gv = gather(va, 0, True)
    gv[0]()

    st_own[...] = jnp.zeros_like(st_own)
    for i, ref in ((0, vq), (1, vk)):
        ins[i].wait()
        for c in range(n // 128):
            st_own[i * 8 + c:i * 8 + c + 1, :] = row_sums(ref[c * 128:(c + 1) * 128, :])
    ins[2].wait()
    ins[3].wait()
    st_own[16:17, :] = row_sums(araw[...].reshape(2 * ar, 256))
    st_copies = []
    for i in range(1, NH):
        c = pltpu.make_async_remote_copy(src_ref=st_own, dst_ref=st_all.at[i - 1], send_sem=st_send.at[i - 1], recv_sem=st_recv.at[i - 1],
                                         device_id={"heads": (hx + i) % NH}, device_id_type=MESH)
        c.start()
        st_copies.append(c)
    for s in gv[1:3]:
        s()
    for c in st_copies:
        c.wait()
    total = st_own[...]
    for i in range(NH - 1):
        total = total + st_all[i]
    scale = lax.rsqrt(total * (1.0 / (HEADS * HD)) + EPS)
    col = along_rows(scale[16:17])
    mine = pl.ds(pl.multiple_of(tok * ar, ar), ar)
    ka[mine, :] = scaled(araw[0], col[0:ar], gak[...])
    qa[mine, :] = scaled(araw[1], col[ar:2 * ar], gaq[...])
    gk = gather(ka, 1, False)
    gq = gather(qa, 2, True)
    gk[0]()
    for s in gv[3:5]:
        s()
    for c in range(n // 128):
        vq[c * 128:(c + 1) * 128, :] = scaled(vq[c * 128:(c + 1) * 128, :], along_rows(scale[c:c + 1]), gvq[...])
        vk[c * 128:(c + 1) * 128, :] = scaled(vk[c * 128:(c + 1) * 128, :], along_rows(scale[8 + c:9 + c]), gvk[...])
    ins[5].wait()
    for c in range(0, n, 256):
        t = jnp.transpose(vv[c:c + 256, :])
        for h in range(4):
            vvT[h, :, c:c + 256] = t[h * HD:(h + 1) * HD]
            voT[h, HD:HD + 16, c:c + 256] = jnp.ones((16, 256), BF)
    rest = [gv[5:], gk[1:]]
    for i in range(max(map(len, rest))):
        for r in rest:
            if i < len(r):
                r[i]()
    for s in gq:
        s()
    for c in range(0, na, 256):
        t = jnp.transpose(va[c:c + 256, :])
        for h in range(4):
            vT[h, 0:HD, c:c + 256] = t[h * HD:(h + 1) * HD]
            vT[h, HD:HD + 16, c:c + 256] = jnp.ones((16, 256), BF)

    factor = HD ** (-0.5) * LOG2E

    def finish1(i, h, row0, acc, m):
        o = acc[0:HD] * (1.0 / acc[HD:HD + 1])
        r = vvT[h, :, pl.ds(row0, TQ)].astype(F32) + o
        voT[h, 0:HD, pl.ds(row0, TQ)] = r.astype(BF)

    attend(4 * (n // TQ), lambda i: (i % 4, pl.multiple_of((i // 4) * TQ, TQ)), ka, vT, vq, na, TK, TQ, factor, (sa, sb), (ma, mb), finish1)
    for c in range(0, n, 256):
        t = jnp.concatenate([voT[h, 0:HD, c:c + 256] for h in range(4)], axis=0)
        vout[c:c + 256, :] = jnp.transpose(t)
    out_copy = pltpu.make_async_copy(vout, vout_h, out_sem)
    out_copy.start()

    slab = na // NX
    per = 4 * (slab // TQ)

    def sl(k):
        return (x0 + (2, 1, 3, 0)[k]) % NX

    x_copies = []
    for k in range(NX):
        xs = sl(k)

        def finish2(i, h, row0, acc, m, k=k, xs=xs):
            o = acc[0:HD] * (1.0 / acc[HD:HD + 1])
            off = pl.multiple_of(row0 - xs * slab, TQ)
            pT[k, pl.ds(pl.multiple_of(h * HD, HD), HD), pl.ds(off, TQ)] = o.astype(BF)
            lse[k, pl.ds(h, 1), pl.ds(off, TQ)] = m + jnp.log2(acc[HD:HD + 1])

        attend(per, lambda i, xs=xs: (i % 4, pl.multiple_of(xs * slab + (i // 4) * TQ, TQ)), vk, voT, qa, n, TK, TQ, factor, (sa, sb), (ma, mb), finish2)
        if k < 3:
            a = pltpu.make_async_remote_copy(src_ref=pT.at[k], dst_ref=xrecv.at[k], send_sem=x_send.at[k], recv_sem=x_recv.at[k],
                                             device_id={"tok": at(xs, z0)}, device_id_type=MESH)
            b = pltpu.make_async_remote_copy(src_ref=lse.at[k], dst_ref=lrecv.at[k], send_sem=xl_send.at[k], recv_sem=xl_recv.at[k],
                                             device_id={"tok": at(xs, z0)}, device_id_type=MESH)
            a.start()
            b.start()
            x_copies += [a, b]
    for c in x_copies:
        c.wait()
    ls = [lrecv[k] for k in range(3)] + [lse[3]]
    top = functools.reduce(jnp.maximum, [l[0:4] for l in ls])
    ws = [jnp.exp2(l[0:4] - top) for l in ls]
    tot = ws[0] + ws[1] + ws[2] + ws[3]
    inv = 1.0 / tot
    lsend[0:4, :] = top + jnp.log2(tot)
    lsend[4:8, :] = jnp.zeros((4, slab), F32)
    ws = [w * inv for w in ws]
    for c in range(0, slab, 256):
        parts = []
        for h in range(4):
            o = pT[3, h * HD:(h + 1) * HD, c:c + 256].astype(F32) * ws[3][h:h + 1, c:c + 256]
            for k in range(3):
                o = o + xrecv[k, h * HD:(h + 1) * HD, c:c + 256].astype(F32) * ws[k][h:h + 1, c:c + 256]
            parts.append(o.astype(BF))
        zsend[c:c + 256, :] = jnp.transpose(jnp.concatenate(parts, axis=0))
    z_copies = []
    for i in range(1, NZ):
        zt = (z0 + i) % NZ
        a = pltpu.make_async_remote_copy(src_ref=zsend.at[pl.ds(pl.multiple_of(zt * ar, ar), ar)], dst_ref=zrecv.at[i - 1],
                                         send_sem=z_send.at[i - 1], recv_sem=z_recv.at[i - 1], device_id={"tok": at(x0, zt)}, device_id_type=MESH)
        b = pltpu.make_async_remote_copy(src_ref=lsend.at[:, pl.ds(pl.multiple_of((zt // 2) * 128, 128), 128)], dst_ref=lzrecv.at[i - 1],
                                         send_sem=zl_send.at[i - 1], recv_sem=zl_recv.at[i - 1], device_id={"tok": at(x0, zt)}, device_id_type=MESH)
        a.start()
        b.start()
        z_copies += [a, b]
    for c in z_copies:
        c.wait()
    ls = [lzrecv[i] for i in range(NZ - 1)] + [lsend[:, pl.ds(pl.multiple_of((z0 // 2) * 128, 128), 128)]]
    top = functools.reduce(jnp.maximum, ls)
    ws = [jnp.exp2(l - top) for l in ls]
    inv = 1.0 / functools.reduce(jnp.add, ws)
    odd = (z0 % 2) == 1
    acc = jnp.zeros((ar, 256), F32)
    for i in range(NZ):
        w = ws[i] * inv
        cols = []
        for h in range(4):
            t = jnp.transpose(jnp.broadcast_to(w[h:h + 1], (128, 128)))
            cols.append(jnp.where(odd, t[ar:2 * ar, 0:HD], t[0:ar, 0:HD]))
        wide = jnp.concatenate(cols, axis=1)
        o = zrecv[i] if i < NZ - 1 else zsend[pl.ds(pl.multiple_of(z0 * ar, ar), ar), :]
        acc = acc + o.astype(F32) * wide
    aout[...] = acc.astype(BF)
    for b, t in ((va, 0), (ka, 1), (qa, 2)):
        drain(b, t)
    out_copy.wait()


def body(video_q, video_k, video_v, audio_q, audio_k, audio_v, video_q_gain, audio_k_gain, audio_q_gain, video_k_gain):
    n, w = video_q.shape
    ar = audio_q.shape[0]
    na = ar * NX * NZ
    slab = na // NX
    A = pl.BlockSpec(memory_space=pl.ANY)
    V = pl.BlockSpec(memory_space=pltpu.VMEM)
    M = pltpu.VMEM
    D = pltpu.SemaphoreType.DMA
    return pl.pallas_call(
        kernel,
        out_shape=(jax.ShapeDtypeStruct((n, w), BF), jax.ShapeDtypeStruct((ar, w), BF)),
        in_specs=[A] * 6 + [V] * 4,
        out_specs=(A, V),
        scratch_shapes=[
            M((n, w), BF), M((n, w), BF), M((n, w), BF), M((2, ar, w), BF), M((na, w), BF), M((na, w), BF), M((na, w), BF),
            M((4, HD + 16, na), BF), M((4, HD + 16, n), BF), M((4, HD, n), BF),
            M((na, TQ), F32), M((na, TQ), F32), M((8, TQ), F32), M((8, TQ), F32),
            M((24, 128), F32), M((NH - 1, 24, 128), F32),
            M((NX, w, slab), BF), M((3, w, slab), BF), M((NX, 8, slab), F32), M((3, 8, slab), F32),
            M((slab, w), BF), M((NZ - 1, ar, w), BF), M((8, slab), F32), M((NZ - 1, 8, 128), F32), M((n, w), BF),
            D((6,)), D, D((NH - 1,)), D((NH - 1,)), D((3,)), D((3, NX * NZ)),
            D((3,)), D((3,)), D((3,)), D((3,)), D((NZ - 1,)), D((NZ - 1,)), D((NZ - 1,)), D((NZ - 1,)),
        ],
        compiler_params=pltpu.CompilerParams(collective_id=0, has_side_effects=True, vmem_limit_bytes=60 * 2**20),
        name="av_cross",
    )(video_q, video_k, video_v, audio_q, audio_k, audio_v, video_q_gain[None], audio_k_gain[None], audio_q_gain[None], video_k_gain[None])


def solution(mesh):
    return jax.shard_map(
        body,
        mesh=mesh,
        in_specs=(P("tok", "heads"),) * 6 + (P("heads"),) * 4,
        out_specs=(P("tok", "heads"), P("tok", "heads")),
        check_vma=False,
    )
```

time: 292 us -> 98.1 us (0.34)
  the two profiles are of different devices: /device:TPU:32 before, /device:TPU:6 now
where the time goes in v1:
time: 98.1 us; the launch traced here: 98 us
  Pallas kernels  94.8 us (97%)
  local copies, waits for them, and re-layouts  2.49 us (3%)
    pallas_call x1, Pallas kernels, body(): pl.pallas_call(kernel, out_shape=(jax.ShapeDtypeStruct((n, w), BF), jax.S...  94.8 us
    unnamed x4, local copies, waits for them, and re-layouts  2.49 us

profile of v1, /device:TPU:6, one launch (start us, length us, event | category | flops | bytes accessed | tf_op | source)
XLA Modules:
  0.0 98.0 jit_solution(8499763761556013093)
XLA Ops:
  0.6 94.8 %av_cross.1 = (bf16[1024,256]{1,0:T(8,128)(2,1)}, bf16[64,256]{1,0:T(8,128)(2,1)}) custom-call(bf16[1024,256]{1,0:T(8,128)(2,1)} %vq_h.1, bf16[1024,256]{1,0:T(8,128)(2,1)} %vk_h.1, bf16[1024,256]{1,0:T(8,128)(2,1)} %vv_h.1, bf16[64,256]{1,0:T(8,128)(2,1)} %aq_h.1, bf16[64,256]{1,0:T(8,128)(2,1)} %ak_h.1, bf16[64,256]{1,0:T(8,128)(2,1)} %av_h.1, ...), custom_call_target="tpu_custom_call" | custom-call | tf_op jit(solution)/shard_map/av_cross/pallas_call | solution.py:352
  95.5 0.0 copy-start
  95.5 1.9 %copy.14 = bf16[1024,256]{1,0:T(8,128)(2,1)} copy(bf16[1024,256]{1,0:T(8,128)(2,1)} %get-tuple-element.4) | data formatting | bytes 1048576
  97.4 0.0 copy-done
  97.4 0.6 copy.15
Async XLA Ops:
  95.5 1.9 %copy-start = (bf16[64,256]{1,0:T(8,128)(2,1)S(1)}, bf16[64,256]{1,0:T(8,128)(2,1)}, u32[]{:S(2)}) copy-start(bf16[64,256]{1,0:T(8,128)(2,1)} %get-tuple-element.5) | copy-start | bytes 98308

commit v2 on v1

v2 whole, which is shorter than its diff:
```python
import functools
import heapq
import jax
import jax.numpy as jnp
from jax import lax
from jax.experimental import pallas as pl
from jax.experimental.pallas import tpu as pltpu
from jax.sharding import PartitionSpec as P

HEADS = 32
HD = 64
EPS = 1e-06
LOG2E = 1.4426950408889634
NX, NZ, NH = 4, 8, 8
NT = (((1,), (1,)), ((), ()))
BF = jnp.bfloat16
F32 = jnp.float32
MESH = pl.DeviceIdType.MESH
TQ = 256
TK = 512

SCHEME = (1, 1, 0, 1, 1, 1)
BLOCK_US, HOP_US, LATE_US = 0.352, 3.3, 2.7


def plan():
    items = len(SCHEME)

    def signed(v, n):
        return v if v <= n // 2 else v - n

    def onward(key):
        t, dx, dz = key
        np_, ns = (NZ, NX) if SCHEME[t] else (NX, NZ)
        p, s = (signed(dz, NZ), signed(dx, NX)) if SCHEME[t] else (signed(dx, NX), signed(dz, NZ))
        hp, hs = np_ // 2, ns // 2
        out = []
        if s == 0:
            if p == 0:
                out += [("p", 1), ("p", -1)]
            elif abs(p) < hp - 1 or p == 1 - hp:
                out.append(("p", -1 if p > 0 else 1))
            out += [("s", 1), ("s", -1)]
        elif abs(s) < hs - 1 or (abs(s) == hs - 1 and (s < 0) == (p % 2 == 0)):
            out.append(("s", -1 if s > 0 else 1))
        return p, s, out

    queue, busy, events, order, count = {}, {}, [], [], 0
    for t in range(items):
        heapq.heappush(events, (0.0 if t < 2 else LATE_US, t, 0, (t, 0, 0)))
    count = items
    while events:
        now, _, kind, x = heapq.heappop(events)
        if kind == 0:
            p, s, out = onward(x)
            for a, d in out:
                link = ("z" if (a == "p") == bool(SCHEME[x[0]]) else "x", d)
                count += 2
                heapq.heappush(queue.setdefault(link, []), (int(x[0] >= 4), int(a == "s"), now, count, x, p, s, a, d))
                heapq.heappush(events, (max(now, busy.get(link, 0.0)), count + 1, 1, link))
        elif queue.get(x):
            if now < busy.get(x, 0.0) - 1e-9:
                count += 1
                heapq.heappush(events, (busy[x], count, 1, x))
                continue
            _, _, _, _, key, p, s, a, d = heapq.heappop(queue[x])
            even_p, even_s = 1 - 2 * (p % 2), 1 - 2 * (s % 2)
            order.append((key[0], even_s * p, even_p * s, a, d * (1 if a == "p" else even_p), now))
            busy[x] = now + BLOCK_US
            t, dx, dz = key
            landed = (t, dx, (dz - x[1]) % NZ) if x[0] == "z" else (t, (dx - x[1]) % NX, dz)
            count += 1
            heapq.heappush(events, (now + BLOCK_US + HOP_US, count, 0, landed))
            count += 1
            heapq.heappush(events, (busy[x], count, 1, x))
    assert len(order) == items * (NX * NZ - 1)
    return order


def make_rhs(x, h, factor):
    x = x.astype(F32) * factor
    lane = lax.broadcasted_iota(jnp.int32, x.shape, 1)
    x = jnp.where((lane // HD) == (h % 2), x, 0.0)
    hi = x.astype(BF)
    lo = (x - hi.astype(F32)).astype(BF)
    return jnp.concatenate([hi, lo], axis=1)


def pair_of(h):
    return pl.ds(pl.multiple_of((h // 2) * 128, 128), 128)


def scores_step(k_ref, h, kt, tk, rhs, s_ref, m):
    pair = pl.multiple_of((h // 2) * 128, 128)
    kk = k_ref[pl.ds(kt * tk, tk), pl.ds(pair, 128)]
    s = lax.dot_general(jnp.concatenate([kk, kk], axis=1), rhs, NT, preferred_element_type=F32)
    s_ref[pl.ds(kt * tk, tk), :] = s
    part = jnp.max(s.reshape(tk // 8, 8, s.shape[1]), axis=0)
    return part if m is None else jnp.maximum(m, part)


def mix_step(v_ref, h, kt, tk, s_ref, m, acc):
    p = jnp.exp2(s_ref[pl.ds(kt * tk, tk), :] - m).astype(BF)
    part = jnp.dot(v_ref[h, :, pl.ds(kt * tk, tk)], p, preferred_element_type=F32)
    return part if acc is None else acc + part


class Pipe:
    def __init__(self, item, k_ref, v_ref, keys, factor, s_refs, m_refs, finish):
        self.item, self.k, self.v, self.keys, self.factor = item, k_ref, v_ref, keys, factor
        self.s, self.m, self.finish = s_refs, m_refs, finish

    def scores(self, i, now, mix=None):
        h, x = self.item(i)
        rhs = make_rhs(x, h, self.factor)
        m, acc = None, None
        for kt in range(self.keys // TK):
            m = scores_step(self.k, h, kt, TK, rhs, self.s[now], m)
            if mix is not None:
                acc = mix_step(self.v, mix[0], kt, TK, self.s[1 - now], mix[1], acc)
        self.m[now][...] = jnp.broadcast_to(jnp.max(m, axis=0, keepdims=True), (8, TQ))
        return acc

    def one(self, i, now):
        prev = self.m[1 - now][0:1]
        h = (i - 1) % 4
        acc = self.scores(i, now, (h, prev))
        self.finish(i - 1, h, acc, prev)

    def last(self, i, now):
        prev = self.m[now][0:1]
        h = i % 4
        acc = None
        for kt in range(self.keys // TK):
            acc = mix_step(self.v, h, kt, TK, self.s[now], prev, acc)
        self.finish(i, h, acc, prev)


def row_sums(x):
    x = x.astype(F32)
    y = x[:, :128] * x[:, :128] + x[:, 128:] * x[:, 128:]
    return jnp.sum(jnp.transpose(y), axis=0, keepdims=True)


def along_rows(row):
    return jnp.transpose(jnp.broadcast_to(row, (128, 128)))


def scaled(x, col, gain):
    c = jnp.concatenate([col, col], axis=1)
    return (x.astype(F32) * c * gain).astype(BF)


def kernel(vq_h, vk_h, vv_h, aq_h, ak_h, av_h, gvq_h, gak_h, gaq_h, gvk_h, vout_h, aout,
           vq, vk, vv, gains, araw, va, ka, qa, vT, voT, vvT, sa, sb, ma, mb,
           sta_own, sta_all, st_own, st_all, pT, xrecv, lse, lrecv, zsend, zrecv, lsend, lzrecv, vout,
           in_sem, out_sem, sta_send, sta_recv, st_send, st_recv, g_send, g_recv, x_send, x_recv, xl_send, xl_recv, z_send, z_recv, zl_send, zl_recv):
    hx = lax.axis_index("heads")
    tok = lax.axis_index("tok")
    x0, z0 = tok // NZ, tok % NZ
    n, na, ar = vq.shape[0], ka.shape[0], araw.shape[1]

    def at(x, z):
        return (x % NX) * NZ + (z % NZ)

    ins = [pltpu.make_async_copy(vq_h, vq, in_sem.at[0]), pltpu.make_async_copy(vk_h, vk, in_sem.at[1]),
           pltpu.make_async_copy(aq_h, araw.at[1], in_sem.at[2]), pltpu.make_async_copy(ak_h, araw.at[0], in_sem.at[3]),
           pltpu.make_async_copy(av_h, va.at[pl.ds(pl.multiple_of(tok * ar, ar), ar)], in_sem.at[4]),
           pltpu.make_async_copy(vv_h, vv, in_sem.at[5])]
    ins += [pltpu.make_async_copy(g, gains.at[i], in_sem.at[6 + i]) for i, g in enumerate((gvq_h, gak_h, gaq_h, gvk_h))]
    for i in (2, 3, 4, 0, 1, 6, 7, 8, 9, 5):
        ins[i].start()

    peers = [{"heads": (hx + i) % NH} for i in range(1, NH)]
    peers += [{"tok": at(x0 + i, z0)} for i in range(1, NX)] + [{"tok": at(x0, z0 + i)} for i in range(1, NZ)]
    barrier = pltpu.get_barrier_semaphore()
    for p in peers:
        pl.semaphore_signal(barrier, inc=1, device_id=p, device_id_type=MESH)
    sta_own[...] = jnp.zeros_like(sta_own)
    ins[2].wait()
    ins[3].wait()
    sta_own[0:1, :] = row_sums(araw[...].reshape(2 * ar, 256))
    ins[4].wait()
    pl.semaphore_wait(barrier, len(peers))

    half = ar // 2
    bufs = (va, va, ka, ka, qa, qa)
    odd_x, odd_z = 1 - 2 * (x0 % 2), 1 - 2 * (z0 % 2)
    order = plan()
    waited = {(t, 0, 0) for t in range(6)}

    def source(t, p, s):
        zf = SCHEME[t]
        sp = (odd_x if zf else odd_z) * (1 - 2 * (s % 2))
        ss = (odd_z if zf else odd_x) * (1 - 2 * (p % 2))
        po, so = sp * p, ss * s
        return at(x0 + so, z0 + po) if zf else at(x0 + po, z0 + so)

    def piece(t, b):
        return bufs[t].at[pl.ds(pl.multiple_of(b * ar + (t % 2) * half, half), half)]

    def arrived(t, p, s):
        np_, ns = (NZ, NX) if SCHEME[t] else (NX, NZ)
        if p == -(np_ // 2):
            p = np_ // 2
        if s == -(ns // 2):
            s = ns // 2
        if (t, p, s) not in waited:
            waited.add((t, p, s))
            b = source(t, p, s)
            ref = piece(t, b)
            pltpu.make_async_copy(ref, ref, g_recv.at[t, b]).wait()

    done = [0]

    def pump(until=None, upto=None):
        while done[0] < len(order):
            t, p, s, a, d, when = order[done[0]]
            if (until is not None and when > until) or (upto is not None and done[0] >= upto):
                return
            arrived(t, p, s)
            zf = SCHEME[t]
            sign = (odd_x if zf else odd_z) if a == "p" else (odd_z if zf else odd_x) * (1 - 2 * (p % 2))
            step = sign * d
            to = at(x0, z0 + step) if (a == "p") == bool(zf) else at(x0 + step, z0)
            b = source(t, p, s)
            ref = piece(t, b)
            pltpu.make_async_remote_copy(src_ref=ref, dst_ref=ref, send_sem=g_send.at[t], recv_sem=g_recv.at[t, b],
                                         device_id={"tok": to}, device_id_type=MESH).start()
            done[0] += 1

    def complete(ts):
        for t in ts:
            np_, ns = (NZ, NX) if SCHEME[t] else (NX, NZ)
            for p in range(1 - np_ // 2, np_ // 2 + 1):
                for s in range(1 - ns // 2, ns // 2 + 1):
                    arrived(t, p, s)

    def to_heads(own, every, send, recv):
        out = []
        for i in range(1, NH):
            c = pltpu.make_async_remote_copy(src_ref=own, dst_ref=every.at[i - 1], send_sem=send.at[i - 1], recv_sem=recv.at[i - 1],
                                             device_id={"heads": (hx + i) % NH}, device_id_type=MESH)
            c.start()
            out.append(c)
        return out

    def scale_of(copies, own, every):
        for c in copies:
            c.wait()
        total = own[...]
        for i in range(NH - 1):
            total = total + every[i]
        return lax.rsqrt(total * (1.0 / (HEADS * HD)) + EPS)

    a_copies = to_heads(sta_own, sta_all, sta_send, sta_recv)
    pump(until=0.1)
    for i, ref in ((0, vq), (1, vk)):
        ins[i].wait()
        for c in range(n // 128):
            st_own[i * 8 + c:i * 8 + c + 1, :] = row_sums(ref[c * 128:(c + 1) * 128, :])
    v_copies = to_heads(st_own, st_all, st_send, st_recv)
    for i in range(6, 10):
        ins[i].wait()
    col = along_rows(scale_of(a_copies, sta_own, sta_all)[0:1])
    mine = pl.ds(pl.multiple_of(tok * ar, ar), ar)
    ka[mine, :] = scaled(araw[0], col[0:ar], gains[1])
    qa[mine, :] = scaled(araw[1], col[ar:2 * ar], gains[2])
    pump(until=LATE_US + 0.4)
    ins[5].wait()
    for c in range(0, n, 256):
        t = jnp.transpose(vv[c:c + 256, :])
        for h in range(4):
            vvT[h, :, c:c + 256] = t[h * HD:(h + 1) * HD]
            voT[h, HD:HD + 16, c:c + 256] = jnp.ones((16, 256), BF)
    pump(until=LATE_US + 1.0)
    scale = scale_of(v_copies, st_own, st_all)
    factor = HD ** (-0.5) * LOG2E
    for qt in range(n // TQ):
        for c in range(qt * TQ // 128, (qt + 1) * TQ // 128):
            vq[c * 128:(c + 1) * 128, :] = scaled(vq[c * 128:(c + 1) * 128, :], along_rows(scale[c:c + 1]), gains[0])
        pump(until=LATE_US + 1.6 + 0.6 * qt)
    for c in range(n // 128):
        vk[c * 128:(c + 1) * 128, :] = scaled(vk[c * 128:(c + 1) * 128, :], along_rows(scale[8 + c:9 + c]), gains[3])

    pump(upto=1 + max(i for i, o in enumerate(order) if o[0] < 4))
    complete((0, 1))
    for c in range(0, na, 256):
        t = jnp.transpose(va[c:c + 256, :])
        for h in range(4):
            vT[h, 0:HD, c:c + 256] = t[h * HD:(h + 1) * HD]
            vT[h, HD:HD + 16, c:c + 256] = jnp.ones((16, 256), BF)
    complete((2, 3))

    def item1(i):
        return i % 4, vq[(i // 4) * TQ:(i // 4 + 1) * TQ, (i % 4 // 2) * 128:(i % 4 // 2 + 1) * 128]

    def finish1(i, h, acc, m):
        r0 = (i // 4) * TQ
        o = acc[0:HD] * (1.0 / acc[HD:HD + 1])
        voT[h, 0:HD, r0:r0 + TQ] = (vvT[h, :, r0:r0 + TQ].astype(F32) + o).astype(BF)

    one = Pipe(item1, ka, vT, na, factor, (sa, sb), (ma, mb), finish1)
    n1 = 4 * (n // TQ)
    left = len(order) - done[0]
    start = done[0]
    one.scores(0, 0)
    for i in range(1, n1):
        pump(upto=start + (left * i) // (n1 - 4))
        one.one(i, i % 2)
    one.last(n1 - 1, (n1 - 1) % 2)
    pump()
    complete((4, 5))

    slab = na // NX

    def slab_of(k):
        o = jnp.where(k == 0, 2, jnp.where(k == 1, 1, jnp.where(k == 2, 3, 0)))
        return (x0 + o) % NX

    def item2(i):
        h, k, hh = i % 4, (i // 4) % 4, i // 16
        base = slab_of(k) * slab + hh * ar
        x = [qa[pl.ds(pl.multiple_of(base + 2 * j * ar, ar), ar), pair_of(h)] for j in range(4)]
        return h, jnp.concatenate(x, axis=0)

    def finish2(i, h, acc, m):
        p = i // 4
        o = acc[0:HD] * (1.0 / acc[HD:HD + 1])
        pT[p, pl.ds(pl.multiple_of(h * HD, HD), HD), :] = o.astype(BF)
        lse[p, pl.ds(h, 1), :] = m + jnp.log2(acc[HD:HD + 1])

    def x_pair(p, k, to):
        a = pltpu.make_async_remote_copy(src_ref=pT.at[p], dst_ref=xrecv.at[p], send_sem=x_send.at[p], recv_sem=x_recv.at[p],
                                         device_id={"tok": at(to, z0)}, device_id_type=MESH)
        b = pltpu.make_async_remote_copy(src_ref=lse.at[p], dst_ref=lrecv.at[p], send_sem=xl_send.at[p], recv_sem=xl_recv.at[p],
                                         device_id={"tok": at(to, z0)}, device_id_type=MESH)
        return a, b

    two = Pipe(item2, vk, voT, n, factor, (sa, sb), (ma, mb), finish2)
    two.scores(0, 0)

    def trip(p, c):
        for j in range(4):
            two.one(4 * p + j + 1, (j + 1) % 2)

        @pl.when(p % 4 < 3)
        def _():
            for c_ in x_pair(p, p % 4, slab_of(p % 4)):
                c_.start()

        return c

    lax.fori_loop(0, 7, trip, 0)
    for j in range(3):
        two.one(29 + j, (j + 1) % 2)
    two.last(31, 1)

    for c in range(0, n, 256):
        t = jnp.concatenate([voT[h, 0:HD, c:c + 256] for h in range(4)], axis=0)
        vout[c:c + 256, :] = jnp.transpose(t)
    out_copy = pltpu.make_async_copy(vout, vout_h, out_sem)
    out_copy.start()

    def z_pair(i):
        zt = (z0 + i) % NZ
        hh, j = zt % 2, zt // 2
        a = pltpu.make_async_remote_copy(src_ref=zsend.at[hh, pl.ds(pl.multiple_of(j * ar, ar), ar)], dst_ref=zrecv.at[i - 1],
                                         send_sem=z_send.at[i - 1], recv_sem=z_recv.at[i - 1], device_id={"tok": at(x0, zt)}, device_id_type=MESH)
        b = pltpu.make_async_remote_copy(src_ref=lsend.at[hh, :, pl.ds(pl.multiple_of((j // 2) * 128, 128), 128)], dst_ref=lzrecv.at[i - 1],
                                         send_sem=zl_send.at[i - 1], recv_sem=zl_recv.at[i - 1], device_id={"tok": at(x0, zt)}, device_id_type=MESH)
        return a, b

    for hh in range(2):
        for k in range(3):
            for c in x_pair(hh * 4 + k, k, slab_of(k)):
                c.wait()
        ls = [lrecv[hh * 4 + k] for k in range(3)] + [lse[hh * 4 + 3]]
        top = functools.reduce(jnp.maximum, [l[0:4] for l in ls])
        ws = [jnp.exp2(l[0:4] - top) for l in ls]
        tot = ws[0] + ws[1] + ws[2] + ws[3]
        inv = 1.0 / tot
        lsend[hh, 0:4, :] = top + jnp.log2(tot)
        lsend[hh, 4:8, :] = jnp.zeros((4, TQ), F32)
        ws = [w * inv for w in ws]
        parts = []
        for h in range(4):
            o = pT[hh * 4 + 3, h * HD:(h + 1) * HD, :].astype(F32) * ws[3][h:h + 1]
            for k in range(3):
                o = o + xrecv[hh * 4 + k, h * HD:(h + 1) * HD, :].astype(F32) * ws[k][h:h + 1]
            parts.append(o.astype(BF))
        zsend[hh] = jnp.transpose(jnp.concatenate(parts, axis=0))
        for j in range(4):
            i = 2 * j + 2 - (z0 + hh) % 2

            @pl.when(i < NZ)
            def _():
                for c in z_pair(i):
                    c.start()

    for i in range(1, NZ):
        for c in z_pair(i):
            c.wait()
    own = z0 % 2
    ls = [lzrecv[i] for i in range(NZ - 1)] + [lsend[own, :, pl.ds(pl.multiple_of((z0 // 4) * 128, 128), 128)]]
    top = functools.reduce(jnp.maximum, ls)
    ws = [jnp.exp2(l - top) for l in ls]
    inv = 1.0 / functools.reduce(jnp.add, ws)
    odd = ((z0 // 2) % 2) == 1
    acc = jnp.zeros((ar, 256), F32)
    for i in range(NZ):
        w = ws[i] * inv
        cols = []
        for h in range(4):
            t = jnp.transpose(jnp.broadcast_to(w[h:h + 1], (128, 128)))
            cols.append(jnp.where(odd, t[ar:2 * ar, 0:HD], t[0:ar, 0:HD]))
        wide = jnp.concatenate(cols, axis=1)
        o = zrecv[i] if i < NZ - 1 else zsend[own, pl.ds(pl.multiple_of((z0 // 2) * ar, ar), ar), :]
        acc = acc + o.astype(F32) * wide
    aout[...] = acc.astype(BF)
    for t in range(6):
        rows = bufs[t].at[pl.ds(0, (NX * NZ - 1) * half)]
        pltpu.make_async_copy(rows, rows, g_send.at[t]).wait()
    out_copy.wait()


def body(video_q, video_k, video_v, audio_q, audio_k, audio_v, video_q_gain, audio_k_gain, audio_q_gain, video_k_gain):
    n, w = video_q.shape
    ar = audio_q.shape[0]
    na = ar * NX * NZ
    A = pl.BlockSpec(memory_space=pl.ANY)
    V = pl.BlockSpec(memory_space=pltpu.VMEM)
    M = pltpu.VMEM
    D = pltpu.SemaphoreType.DMA
    return pl.pallas_call(
        kernel,
        out_shape=(jax.ShapeDtypeStruct((n, w), BF), jax.ShapeDtypeStruct((ar, w), BF)),
        in_specs=[A] * 10,
        out_specs=(A, V),
        scratch_shapes=[
            M((n, w), BF), M((n, w), BF), M((n, w), BF), M((4, 1, w), F32), M((2, ar, w), BF), M((na, w), BF), M((na, w), BF), M((na, w), BF),
            M((4, HD + 16, na), BF), M((4, HD + 16, n), BF), M((4, HD, n), BF),
            M((na, TQ), F32), M((na, TQ), F32), M((8, TQ), F32), M((8, TQ), F32),
            M((8, 128), F32), M((NH - 1, 8, 128), F32), M((16, 128), F32), M((NH - 1, 16, 128), F32),
            M((8, w, TQ), BF), M((8, w, TQ), BF), M((8, 8, TQ), F32), M((8, 8, TQ), F32),
            M((2, TQ, w), BF), M((NZ - 1, ar, w), BF), M((2, 8, TQ), F32), M((NZ - 1, 8, 128), F32), M((n, w), BF),
            D((10,)), D, D((NH - 1,)), D((NH - 1,)), D((NH - 1,)), D((NH - 1,)), D((6,)), D((6, NX * NZ)),
            D((8,)), D((8,)), D((8,)), D((8,)), D((NZ - 1,)), D((NZ - 1,)), D((NZ - 1,)), D((NZ - 1,)),
        ],
        compiler_params=pltpu.CompilerParams(collective_id=0, has_side_effects=True, vmem_limit_bytes=60 * 2**20),
        name="av_cross",
    )(video_q, video_k, video_v, audio_q, audio_k, audio_v, video_q_gain[None], audio_k_gain[None], audio_q_gain[None], video_k_gain[None])


def solution(mesh):
    return jax.shard_map(
        body,
        mesh=mesh,
        in_specs=(P("tok", "heads"),) * 6 + (P("heads"),) * 4,
        out_specs=(P("tok", "heads"), P("tok", "heads")),
        check_vma=False,
    )
```

time: 98.1 us -> 74 us (0.75)
  the two profiles are of different devices: /device:TPU:6 before, /device:TPU:32 now
where the time goes in v2:
time: 74 us; the launch traced here: 73.9 us
  Pallas kernels  70.7 us (96%)
  local copies, waits for them, and re-layouts  2.49 us (3%)
    pallas_call x1, Pallas kernels, body(): pl.pallas_call(kernel, out_shape=(jax.ShapeDtypeStruct((n, w), BF), jax.S...  70.7 us
    unnamed x4, local copies, waits for them, and re-layouts  2.49 us

profile of v2, /device:TPU:32, one launch (start us, length us, event | category | flops | bytes accessed | tf_op | source)
XLA Modules:
  0.0 73.9 jit_solution(1700326310638397868)
XLA Ops:
  0.6 70.7 %av_cross.1 = (bf16[1024,256]{1,0:T(8,128)(2,1)}, bf16[64,256]{1,0:T(8,128)(2,1)}) custom-call(bf16[1024,256]{1,0:T(8,128)(2,1)} %vq_h.1, bf16[1024,256]{1,0:T(8,128)(2,1)} %vk_h.1, bf16[1024,256]{1,0:T(8,128)(2,1)} %vv_h.1, bf16[64,256]{1,0:T(8,128)(2,1)} %aq_h.1, bf16[64,256]{1,0:T(8,128)(2,1)} %ak_h.1, bf16[64,256]{1,0:T(8,128)(2,1)} %av_h.1, ...), custom_call_target="tpu_custom_call" | custom-call | tf_op jit(solution)/shard_map/av_cross/pallas_call | solution.py:435
  71.4 0.0 copy-start
  71.4 1.9 %copy.14 = bf16[1024,256]{1,0:T(8,128)(2,1)} copy(bf16[1024,256]{1,0:T(8,128)(2,1)} %get-tuple-element.4) | data formatting | bytes 1048576
  73.3 0.0 copy-done
  73.3 0.6 copy.15
Async XLA Ops:
  71.4 1.9 %copy-start = (bf16[64,256]{1,0:T(8,128)(2,1)S(1)}, bf16[64,256]{1,0:T(8,128)(2,1)}, u32[]{:S(2)}) copy-start(bf16[64,256]{1,0:T(8,128)(2,1)} %get-tuple-element.5) | copy-start | bytes 98308

commit v3 on v2

--- a/solution.py
+++ b/solution.py
@@ -19,8 +19,8 @@
 TQ = 256
 TK = 512
 
-SCHEME = (1, 1, 0, 1, 1, 1)
-BLOCK_US, HOP_US, LATE_US = 0.352, 3.3, 2.7
+SCHEME = (1, 1, 1, 0, 1, 0)
+BLOCK_US, HOP_US, LATE_US, FAR_US = 0.352, 3.3, 3.5, 0.75
 
 
 def plan():
@@ -33,19 +33,22 @@
         t, dx, dz = key
         np_, ns = (NZ, NX) if SCHEME[t] else (NX, NZ)
         p, s = (signed(dz, NZ), signed(dx, NX)) if SCHEME[t] else (signed(dx, NX), signed(dz, NZ))
-        hp, hs = np_ // 2, ns // 2
         out = []
         if s == 0:
             if p == 0:
-                out += [("p", 1), ("p", -1)]
-            elif abs(p) < hp - 1 or p == 1 - hp:
-                out.append(("p", -1 if p > 0 else 1))
-            out += [("s", 1), ("s", -1)]
-        elif abs(s) < hs - 1 or (abs(s) == hs - 1 and (s < 0) == (p % 2 == 0)):
-            out.append(("s", -1 if s > 0 else 1))
+                out += [("p", d) for d in range(np_ // 2, -((np_ + 1) // 2), -1) if d not in (0, -np_ // 2)]
+            out += [("s", d) for d in ((1, -1) if ns == 4 else (2, -2, 1, -1))]
+        else:
+            back = -1 if s > 0 else 1
+            side = (s < 0) == (p % 2 == 0)
+            if abs(s) == ns // 4:
+                if ns == 8:
+                    out.append(("s", back))
+                if side:
+                    out.append(("s", back * ns // 4))
         return p, s, out
 
-    queue, busy, events, order, count = {}, {}, [], [], 0
+    queue, busy, events, order, count, land = {}, {}, [], [], 0, {}
     for t in range(items):
         heapq.heappush(events, (0.0 if t < 2 else LATE_US, t, 0, (t, 0, 0)))
     count = items
@@ -53,24 +56,32 @@
         now, _, kind, x = heapq.heappop(events)
         if kind == 0:
             p, s, out = onward(x)
+            cz, cx = ((1 - 2 * (s % 2)) * p, (1 - 2 * (p % 2)) * s) if SCHEME[x[0]] else ((1 - 2 * (p % 2)) * s, (1 - 2 * (s % 2)) * p)
+            cz, cx = (NZ // 2 if cz == -(NZ // 2) else cz), (NX // 2 if cx == -(NX // 2) else cx)
+            if x[0] < 4:
+                land[cx, cz] = max(land.get((cx, cz), 0.0), now)
             for a, d in out:
-                link = ("z" if (a == "p") == bool(SCHEME[x[0]]) else "x", d)
+                link = ("z" if (a == "p") == bool(SCHEME[x[0]]) else "x", 1 if d > 0 else -1)
                 count += 2
-                heapq.heappush(queue.setdefault(link, []), (int(x[0] >= 4), int(a == "s"), now, count, x, p, s, a, d))
+                heapq.heappush(queue.setdefault(link, []), (int(x[0] >= 4), int(a == "s"), -abs(d), now, count, x, p, s, a, d))
                 heapq.heappush(events, (max(now, busy.get(link, 0.0)), count + 1, 1, link))
         elif queue.get(x):
             if now < busy.get(x, 0.0) - 1e-9:
                 count += 1
                 heapq.heappush(events, (busy[x], count, 1, x))
                 continue
-            _, _, _, _, key, p, s, a, d = heapq.heappop(queue[x])
-            even_p, even_s = 1 - 2 * (p % 2), 1 - 2 * (s % 2)
-            order.append((key[0], even_s * p, even_p * s, a, d * (1 if a == "p" else even_p), now))
-            busy[x] = now + BLOCK_US
+            _, _, _, _, _, key, p, s, a, d = heapq.heappop(queue[x])
+            even_p = 1 - 2 * (p % 2)
+            order.append((key[0], (1 - 2 * (s % 2)) * p, even_p * s, a, d * (1 if a == "p" else even_p), now))
+            both = 2 * abs(d) == (NZ if x[0] == "z" else NX)
+            wire = BLOCK_US * abs(d) * (0.5 if both else 1.0)
+            busy[x] = now + wire
+            if both:
+                busy[x[0], -x[1]] = max(busy.get((x[0], -x[1]), 0.0), now) + wire
             t, dx, dz = key
-            landed = (t, dx, (dz - x[1]) % NZ) if x[0] == "z" else (t, (dx - x[1]) % NX, dz)
+            landed = (t, dx, (dz - d) % NZ) if x[0] == "z" else (t, (dx - d) % NX, dz)
             count += 1
-            heapq.heappush(events, (now + BLOCK_US + HOP_US, count, 0, landed))
+            heapq.heappush(events, (now + wire + HOP_US + FAR_US * (abs(d) - 1), count, 0, landed))
             count += 1
             heapq.heappush(events, (busy[x], count, 1, x))
     assert len(order) == items * (NX * NZ - 1)

time: 74 us -> 73.2 us (0.989)
  Pallas kernels: 70.7 us -> 69.9 us
    pallas_call x1, Pallas kernels: 70.7 us -> 69.9 us  [body(): pl.pallas_call(kernel, out_shape=(jax.ShapeDtypeStruct((n, w), BF), jax.S...]
where the time goes in v3:
time: 73.2 us; the launch traced here: 73.1 us
  Pallas kernels  69.9 us (95%)
  local copies, waits for them, and re-layouts  2.49 us (3%)
    pallas_call x1, Pallas kernels, body(): pl.pallas_call(kernel, out_shape=(jax.ShapeDtypeStruct((n, w), BF), jax.S...  69.9 us
    unnamed x4, local copies, waits for them, and re-layouts  2.49 us

profile of v3, /device:TPU:32, one launch (start us, length us, event | category | flops | bytes accessed | tf_op | source)
XLA Modules:
  0.0 73.1 jit_solution(6511494139902474805)
XLA Ops:
  0.6 69.9 %av_cross.1 = (bf16[1024,256]{1,0:T(8,128)(2,1)}, bf16[64,256]{1,0:T(8,128)(2,1)}) custom-call(bf16[1024,256]{1,0:T(8,128)(2,1)} %vq_h.1, bf16[1024,256]{1,0:T(8,128)(2,1)} %vk_h.1, bf16[1024,256]{1,0:T(8,128)(2,1)} %vv_h.1, bf16[64,256]{1,0:T(8,128)(2,1)} %aq_h.1, bf16[64,256]{1,0:T(8,128)(2,1)} %ak_h.1, bf16[64,256]{1,0:T(8,128)(2,1)} %av_h.1, ...), custom_call_target="tpu_custom_call" | custom-call | tf_op jit(solution)/shard_map/av_cross/pallas_call | solution.py:446
  70.6 0.0 copy-start
  70.6 1.9 %copy.14 = bf16[1024,256]{1,0:T(8,128)(2,1)} copy(bf16[1024,256]{1,0:T(8,128)(2,1)} %get-tuple-element.4) | data formatting | bytes 1048576
  72.4 0.0 copy-done
  72.4 0.6 copy.15
Async XLA Ops:
  70.6 1.9 %copy-start = (bf16[64,256]{1,0:T(8,128)(2,1)S(1)}, bf16[64,256]{1,0:T(8,128)(2,1)}, u32[]{:S(2)}) copy-start(bf16[64,256]{1,0:T(8,128)(2,1)} %get-tuple-element.5) | copy-start | bytes 98308

commit v4 on v3

--- a/solution.py
+++ b/solution.py
@@ -317,7 +317,7 @@
     start = done[0]
     one.scores(0, 0)
     for i in range(1, n1):
-        pump(upto=start + (left * i) // (n1 - 4))
+        pump(upto=start + (left * i) // (n1 - 6))
         one.one(i, i % 2)
     one.last(n1 - 1, (n1 - 1) % 2)
     pump()

time: 73.2 us -> 72.7 us (level)
  no operation moved by 1% of the time
where the time goes in v4:
time: 72.7 us; the launch traced here: 72.6 us
  Pallas kernels  69.5 us (96%)
  local copies, waits for them, and re-layouts  2.49 us (3%)
    pallas_call x1, Pallas kernels, body(): pl.pallas_call(kernel, out_shape=(jax.ShapeDtypeStruct((n, w), BF), jax.S...  69.5 us
    unnamed x4, local copies, waits for them, and re-layouts  2.49 us

profile of v4, /device:TPU:32, one launch (start us, length us, event | category | flops | bytes accessed | tf_op | source)
XLA Modules:
  0.0 72.6 jit_solution(3346444542225433853)
XLA Ops:
  0.6 69.5 %av_cross.1 = (bf16[1024,256]{1,0:T(8,128)(2,1)}, bf16[64,256]{1,0:T(8,128)(2,1)}) custom-call(bf16[1024,256]{1,0:T(8,128)(2,1)} %vq_h.1, bf16[1024,256]{1,0:T(8,128)(2,1)} %vk_h.1, bf16[1024,256]{1,0:T(8,128)(2,1)} %vv_h.1, bf16[64,256]{1,0:T(8,128)(2,1)} %aq_h.1, bf16[64,256]{1,0:T(8,128)(2,1)} %ak_h.1, bf16[64,256]{1,0:T(8,128)(2,1)} %av_h.1, ...), custom_call_target="tpu_custom_call" | custom-call | tf_op jit(solution)/shard_map/av_cross/pallas_call | solution.py:446
  70.1 0.0 copy-start
  70.1 1.9 %copy.14 = bf16[1024,256]{1,0:T(8,128)(2,1)} copy(bf16[1024,256]{1,0:T(8,128)(2,1)} %get-tuple-element.4) | data formatting | bytes 1048576
  72.0 0.0 copy-done
  72.0 0.6 copy.15
Async XLA Ops:
  70.1 1.9 %copy-start = (bf16[64,256]{1,0:T(8,128)(2,1)S(1)}, bf16[64,256]{1,0:T(8,128)(2,1)}, u32[]{:S(2)}) copy-start(bf16[64,256]{1,0:T(8,128)(2,1)} %get-tuple-element.5) | copy-start | bytes 98308
